TPU v7x, 32 devices: a whole 2x2x4 slice. The times are simulated.
32 devices in a mesh: row: 4 (over z), col: 8 (over y, x, core).
Axes of the slice: x: 2, y: 2, z: 4, core: 2. Of those that a mesh axis runs over, the one named last changes fastest.
Arguments:
- inverse_interior: float32 [4, 8, 1536, 1536], P('row', 'col'), may hold values from -0.15625 to 0.15625
- coupling: float32 [4, 8, 1536, 1024], P('row', 'col'), may hold values from -1 to 1
- interface_block: float32 [4, 8, 1024, 1024], P('row', 'col'), may hold values from -6 to 6
- iface_ids: int32 [4, 8, 4], P('row', 'col'), may hold values from 0 to 7, as said below
- row_place: int32 [8], replicated, may hold values from 0 to 7, as said below
- col_place: int32 [8], replicated, may hold values from 0 to 7, as said below
Outputs:
- assembled: float32 [8, 256, 8, 256], P('row', None, 'col')
Inputs may be any that keep to these rules, and one draw needn't show every extreme that they name: `row_place`: A permutation of the tile ids. `col_place`: a permutation of the tile ids; two ids whose values of row_place differ mod 4 have values of col_place that differ mod 8. `iface_ids`: the 4 ids of one subdomain have pairwise different row_place mod 4, hence pairwise different col_place mod 8.
All inputs are finite; a program needn't handle non-finite values.
Results may differ from a plain program's by a relative error of at most 0.0001.
Values sent between devices are 32-bit elements; how exact they have to be, the bound alone decides.
A program may use at most 192 MiB of HBM per device.

v0:
```python
import jax
import jax.numpy as jnp
from jax import lax
from jax.sharding import PartitionSpec as P

TILE = 256


def on_device(inverse_interior, coupling, interface_block, iface_ids, row_place, col_place):
    high = lax.Precision.HIGH
    f32 = jnp.float32
    rows = lax.axis_size("row")
    cols = lax.axis_size("col")
    total_ids = row_place.shape[0]
    slots = total_ids // rows
    own_cols = total_ids // cols
    spread = cols // rows
    part = TILE // spread
    count = coupling.shape[3] // TILE
    c = coupling[0, 0]
    solved = jnp.dot(inverse_interior[0, 0], c, precision=high, preferred_element_type=f32)
    product = lax.dot_general(c, solved, (((0,), (0,)), ((), ())), precision=high, preferred_element_type=f32)
    schur = interface_block[0, 0] - product
    ids = iface_ids[0, 0]
    matches = ids[:, None] == jnp.arange(total_ids, dtype=jnp.int32)[None, :]
    pos = jnp.sum(jnp.where(matches, row_place[None, :], 0), axis=1)
    group = pos % rows
    hit = group[None, :] == jnp.arange(rows, dtype=jnp.int32)[:, None]
    local = jnp.sum(jnp.where(hit, jnp.arange(count, dtype=jnp.int32)[None, :], 0), axis=1)
    slot = jnp.sum(jnp.where(hit, pos[None, :] // rows + 1, 0), axis=1) - 1
    strips = jnp.stack([lax.dynamic_slice_in_dim(schur, local[p] * TILE, TILE, 0) for p in range(rows)])
    out = jnp.stack([lax.dynamic_slice_in_dim(strips, local[q] * TILE, TILE, 2) for q in range(rows)])
    out = out.reshape(rows, rows, spread, part, TILE).transpose(0, 2, 1, 3, 4).reshape(cols, rows, part, TILE)
    arrived = lax.all_to_all(out, "col", split_axis=0, concat_axis=0, tiled=True)
    codes = lax.all_gather(slot.astype(f32), "col")
    mine = lax.axis_index("col") // spread
    own_code = jnp.sum(jnp.where(jnp.arange(rows)[None, :] == mine, codes, 0.0), axis=1)
    table = jnp.arange(slots).astype(f32)
    row_hit = codes[:, :, None] == table
    col_hit = own_code[:, None] == table
    mask = row_hit[:, :, :, None] & col_hit[:, None, None, :]
    total = jnp.sum(
        jnp.where(mask[:, :, :, :, None, None], arrived[:, :, None, None], 0.0), axis=0
    )
    summed = lax.psum_scatter(total, "row", scatter_dimension=0, tiled=True)[0]
    gathered = lax.all_gather(summed, "col")
    gathered = gathered.reshape(rows, spread, slots, slots, part, TILE)
    pieces = []
    for u in range(own_cols):
        want = u * cols + lax.axis_index("col")
        place = jnp.sum(jnp.where(col_place == want, row_place, 0))
        piece = lax.dynamic_slice(
            gathered,
            (place % rows, 0, 0, place // rows, 0, 0),
            (1, spread, slots, 1, part, TILE),
        )
        pieces.append(piece[0, :, :, 0].transpose(1, 0, 2, 3).reshape(slots, TILE, TILE))
    return jnp.stack(pieces, axis=2)


def solution(mesh):
    return jax.shard_map(
        on_device,
        mesh=mesh,
        in_specs=(
            P("row", "col", None, None),
            P("row", "col", None, None),
            P("row", "col", None, None),
            P("row", "col", None),
            P(),
            P(),
        ),
        out_specs=P("row", None, "col", None),
        check_vma=False,
    )
```

profile of v0, /device:TPU:9, one launch (start us, length us, event | category | flops | bytes accessed | tf_op | source)
XLA Modules:
  0.0 218.6 jit_solution(6577536210472001047)
XLA Ops:
  6.5 0.9 select_reduce_fusion.4
  7.4 0.1 select_reduce_fusion.3
  7.6 0.7 fusion.10
  10.8 0.0 slice-start
  10.8 5.5 %copy.32 = f32[1,1,1024,1024]{2,3,1,0:T(8,128)} copy(f32[1,1,1024,1024]{3,2,1,0:T(8,128)} %param.8) | data formatting | bytes 8388608 | tf_op args[2]
  16.3 0.0 copy-start
  16.3 0.0 slice-start.1
  16.3 18.2 %fusion = f32[1536,1024]{1,0:T(8,128)S(1)} fusion(f32[1,1,1536,1536]{3,2,1,0:T(8,128)} %param.6, f32[1,1,1536,1024]{3,2,1,0:T(8,128)} %param.7), kind=kOutput, calls=%fused_computation.1 | convolution fusion | flops 14495514624 | bytes 22020096 | tf_op jit(solution)/shard_map/dot_general | solution.py:21
  34.5 0.0 slice-done
  34.5 0.0 copy-done
  34.5 0.0 slice-done.1
  34.5 11.5 %bitcast_subtract_fusion = f32[1024,1024]{0,1:T(8,128)} fusion(f32[1,1,1024,1024]{2,3,1,0:T(8,128)S(1)} %copy-done, f32[1536,1024]{1,0:T(8,128)S(1)} %fusion, f32[1,1,1536,1024]{3,2,1,0:T(8,128)S(1)} %bitcast.48), kind=kOutput, calls=%fused_computation.9 | convolution fusion | flops 9664724992 | bytes 20971520 | tf_op jit(solution)/shard_map/dot_general | solution.py:22
  46.1 2.5 %dynamic-slice_bitcast_fusion.3 = (f32[1,256,1024]{1,2,0:T(8,128)S(1)}, f32[1,256,1024]{1,2,0:T(8,128)S(1)}, f32[1,256,1024]{1,2,0:T(8,128)S(1)}, f32[1,256,1024]{1,2,0:T(8,128)S(1)}) fusion(f32[1024,1024]{0,1:T(8,128)} %bitcast_subtract_fusion, s32[]{:T(128)S(6)} %select_n.86, s32[]{:T(128)S(6)} %select_n.89, s32[]{:T(128)S(6)} %select_n.88, s32[]{:T(128)S(6)} %select_n.87), kind=kLoop, calls=%fused_computation.13 | loop fusion | bytes 8388624 | tf_op jit(solution)/shard_map/stack | solution.py:31
  48.6 0.4 pad_maximum_fusion
  48.9 1.4 constant_dynamic-slice_fusion.3
  50.4 2.5 %copy.36 = f32[4,256,256]{2,1,0:T(8,128)} copy(f32[4,256,256]{1,2,0:T(8,128)} %get-tuple-element.10) | data formatting | bytes 2097152 | tf_op jit(solution)/shard_map/dynamic_slice | solution.py:32
  52.9 1.4 copy.35
  54.3 1.3 copy.34
  55.6 0.3 copy.33
  56.0 0.0 copy-done.1
  56.0 1.9 pad_maximum_fusion.1
  57.9 0.3 fusion.9
  58.2 2.2 %pad_maximum_fusion.2 = f32[4,8,128,256]{3,2,1,0:T(8,128)} fusion(f32[4,4,128,256]{3,2,1,0:T(8,128)S(1)} %get-tuple-element.8, f32[4,4,128,256]{3,2,1,0:T(8,128)S(1)} %get-tuple-element.7), kind=kLoop, calls=%fused_computation.8 | loop fusion | flops 1048576 | bytes 8388608 | tf_op jit(solution)/shard_map/concatenate
  60.5 5.2 %all-to-all-start = ((f32[8,4,128,256]{3,2,1,0:T(8,128)}), f32[8,4,128,256]{3,2,1,0:T(8,128)}, u32[]{:S(2)}, u32[]{:S(2)}) async-start(f32[8,4,128,256]{3,2,1,0:T(8,128)} %bitcast.40), calls=%async_computation | async-start | bytes 8388608 | tf_op jit(solution)/shard_map/all_to_all | solution.py:34
  65.7 0.0 reduce-scatter.2.cloned.1.call-start
  65.7 0.0 copy-done.4
  65.7 0.6 dynamic-slice
  66.9 0.1 convert_dynamic-update-slice_fusion
  67.0 53.3 %all-reduce = f32[32]{0:T(128)S(1)} all-reduce(f32[32]{0:T(128)S(1)} %convert_dynamic-update-slice_fusion), channel_id=2, replica_groups=mesh['row'=4,'col'=8] {'col'}, use_global_device_ids=true, to_apply=%add | all-reduce | flops 32 | bytes 256
  120.3 0.1 reshape.122
  120.4 0.1 select_reduce_fusion.1
  120.5 0.1 broadcast_compare_fusion.1
  120.6 0.1 broadcast_compare_fusion
  120.7 0.1 broadcast_and_fusion
  120.8 0.0 copy-start.2
  120.8 0.0 copy-start.3
  120.8 0.0 all-to-all-done
  120.8 5.9 %select_reduce_fusion = f32[4,2,2,128,256]{4,3,2,1,0:T(8,128)} fusion(f32[8,4,128,256]{3,2,1,0:T(8,128)} %all-to-all-done, pred[8,4,2,2]{3,2,1,0:T(4,128)(4,1)S(1)} %broadcast_and_fusion), kind=kLoop, calls=%fused_computation | loop fusion | flops 7864320 | bytes 6291584 | tf_op jit(solution)/shard_map/reduce_sum | solution.py:42
  126.7 0.0 reduce-scatter.2.cloned.1.call-update
  126.8 0.0 all-gather.3.cloned.1.call-start
  126.8 42.5 %reduce-scatter.2.cloned.1.call-done = f32[1,2,2,128,256]{4,3,2,1,0:T(8,128)} async-done(((f32[4,2,2,128,256]{4,3,2,1,0:T(8,128)}), f32[1,2,2,128,256]{4,3,2,1,0:T(8,128)}) %reduce-scatter.2.cloned.1.call-update) | async-done | bytes 524304 | tf_op jit(solution)/shard_map/reduce_scatter | solution.py:45
  169.3 0.0 all-gather.3.cloned.1.call-update
  169.3 0.0 copy-done.2
  169.3 0.0 copy-done.3
  169.3 0.6 fusion.7
  172.6 36.8 %all-gather.3.cloned.1.call-done = f32[8,2,2,128,256]{4,3,2,1,0:T(8,128)} async-done(((f32[1,2,2,128,256]{4,3,2,1,0:T(8,128)}), f32[8,2,2,128,256]{4,3,2,1,0:T(8,128)}) %all-gather.3.cloned.1.call-update) | async-done | bytes 4194320 | tf_op jit(solution)/shard_map/all_gather | solution.py:46
  209.4 1.1 dynamic-slice_bitcast_fusion.4
  210.5 1.3 copy.38
  (8 shorter events, 0.1 us)
Async XLA Ops:
  10.8 23.7 %slice-start = ((s8[6291456]{0:T(1024)(128)(4,1)}), s8[2097152]{0:T(1024)(128)(4,1)S(1)}, s32[]{:S(2)}) async-start(s8[6291456]{0:T(1024)(128)(4,1)} %bitcast.47), calls=%async_computation.4 | async-start | bytes 4194304
  16.3 18.2 %copy-start = (f32[1,1,1024,1024]{2,3,1,0:T(8,128)S(1)}, f32[1,1,1024,1024]{2,3,1,0:T(8,128)}, u32[]{:S(2)}) copy-start(f32[1,1,1024,1024]{2,3,1,0:T(8,128)} %copy.32) | copy-start | bytes 12582916
  16.3 18.2 %slice-start.1 = ((s8[6291456]{0:T(1024)(128)(4,1)}), s8[4194304]{0:T(1024)(128)(4,1)S(1)}, s32[]{:S(2)}) async-start(s8[6291456]{0:T(1024)(128)(4,1)} %bitcast.47), calls=%async_computation.5 | async-start | bytes 8388608
  54.3 1.7 copy-start.1
  60.5 5.2 %copy-start.4 = (u32[32]{0:T(128)S(1)}, u32[32]{0:T(128)}, u32[]{:S(2)}) copy-start(u32[32]{0:T(128)} %constant.76) | copy-start | bytes 388
  60.5 60.3 %all-to-all-start = ((f32[8,4,128,256]{3,2,1,0:T(8,128)}), f32[8,4,128,256]{3,2,1,0:T(8,128)}, u32[]{:S(2)}, u32[]{:S(2)}) async-start(f32[8,4,128,256]{3,2,1,0:T(8,128)} %bitcast.40), calls=%async_computation | async-start | bytes 8388608 | tf_op jit(solution)/shard_map/all_to_all | solution.py:34
  65.7 103.6 %reduce-scatter.2.cloned.1.call-start = ((), (), s32[]{:S(2)}) async-start(), calls=%async_computation.2 | async-start | bytes 2621440 | tf_op jit(solution)/shard_map/reduce_scatter | solution.py:45
  120.8 48.6 %copy-start.2 = (s32[8]{0:T(128)S(1)}, s32[8]{0:T(128)}, u32[]{:S(2)}) copy-start(s32[8]{0:T(128)} %param.10) | copy-start | bytes 100
  120.8 48.6 %copy-start.3 = (s32[8]{0:T(128)S(1)}, s32[8]{0:T(128)}, u32[]{:S(2)}) copy-start(s32[8]{0:T(128)} %param.11) | copy-start | bytes 100
  126.8 82.6 %all-gather.3.cloned.1.call-start = ((), (), s32[]{:S(2)}) async-start(), calls=%async_computation.3 | async-start | bytes 4718592 | tf_op jit(solution)/shard_map/all_gather | solution.py:46
Sparse Core Ops, SparseCore 0:
  126.9 42.3 reduce-scatter.1
  171.2 38.1 all-gather.2
where the time goes:
time: 220 us; the launch traced here: 219 us
  waiting for transfers between devices  79.3 us (36%)
  blocking collectives  53.3 us (24%)
  matrix products  29.7 us (14%)
  between operations  19.4 us (9%)
  local copies, waits for them, and re-layouts  19.1 us (9%)
  other arithmetic  12.6 us (6%)
  starting transfers between devices  5.27 us (2%)
    unnamed x1, blocking collectives  53.3 us
    reduce_scatter x1, waiting for transfers between devices, on_device(): summed = lax.psum_scatter(total, 'row', scatter_dimension=0, tiled=True)[0]  42.5 us
    all_gather x1, waiting for transfers between devices, on_device(): gathered = lax.all_gather(summed, 'col')  36.8 us
    dot_general x1, matrix products, on_device(): jnp.dot(inverse_interior[0, 0], c, precision=high, preferred_element_type...  18.2 us
    dot_general x1, matrix products, on_device(): lax.dot_general(c, solved, (((0,), (0,)), ((), ())), precision=high, pref...  11.5 us
    dynamic_slice x5, local copies, waits for them, and re-layouts, on_device(): lax.dynamic_slice_in_dim(strips, local[q] * TILE, TILE, 2)  7.02 us
    unnamed x17, local copies, waits for them, and re-layouts  6.13 us
    reduce_sum x1, other arithmetic, on_device(): jnp.sum(jnp.where(mask[:, :, :, :, None, None], arrived[:, :, None, None]...  5.94 us
  transfers between devices with their start and end apart: 3, of which 2 were waited for; matrix products, arithmetic and copies ran while one was open for 1% of the time, Pallas kernels for 0%

commit v1 on v0

--- a/solution.py
+++ b/solution.py
@@ -1,12 +1,16 @@
+import functools
+
 import jax
 import jax.numpy as jnp
 from jax import lax
+from jax.experimental import pallas as pl
+from jax.experimental.pallas import tpu as pltpu
 from jax.sharding import PartitionSpec as P
 
 TILE = 256
 
 
-def on_device(inverse_interior, coupling, interface_block, iface_ids, row_place, col_place):
+def general(inverse_interior, coupling, interface_block, iface_ids, row_place, col_place):
     high = lax.Precision.HIGH
     f32 = jnp.float32
     rows = lax.axis_size("row")
@@ -58,6 +62,225 @@
     return jnp.stack(pieces, axis=2)
 
 
+def assemble(
+    rows, cols, slots, own_cols,
+    place_ref, code_ref, th_ref, tl_ref, ch_ref, cl_ref, block_ref,
+    out_ref,
+    tiles, landed, codes, acc, row_landed, final, stage, pair_landed,
+    code_send, code_recv, tile_send, tile_recv, row_send, row_recv, all_send, all_recv, pair_send, pair_recv,
+):
+    spread = cols // rows
+    part = TILE // spread
+    groups = part // 8
+    z = lax.axis_index("row")
+    d = lax.axis_index("col")
+    mine = lax.div(d, spread)
+    k = lax.rem(d, spread)
+
+    def remote(src, dst, send, recv, row, col):
+        return pltpu.make_async_remote_copy(
+            src_ref=src, dst_ref=dst, send_sem=send, recv_sem=recv,
+            device_id=(row, col), device_id_type=pl.DeviceIdType.MESH,
+        )
+
+    barrier = pltpu.get_barrier_semaphore()
+    for o in range(1, cols):
+        pl.semaphore_signal(
+            barrier, inc=1, device_id=(z, lax.rem(d + o, cols)), device_id_type=pl.DeviceIdType.MESH
+        )
+    for o in range(1, rows):
+        pl.semaphore_signal(
+            barrier, inc=1, device_id=(lax.rem(z + o, rows), d), device_id_type=pl.DeviceIdType.MESH
+        )
+
+    started = []
+    code_copies = {}
+    tile_copies = {}
+    for j in range(rows):
+        p = lax.rem(z + 1 + j, rows)
+        strip = pl.ds(pl.multiple_of(p * TILE, TILE), TILE)
+
+        @pl.loop(0, rows)
+        def _(q, j=j, strip=strip):
+            band = pl.ds(pl.multiple_of(q * TILE, TILE), TILE)
+            f32 = jnp.float32
+            product = (
+                jnp.dot(tl_ref[strip, :], ch_ref[:, band], preferred_element_type=f32)
+                + jnp.dot(th_ref[strip, :], cl_ref[:, band], preferred_element_type=f32)
+                + jnp.dot(th_ref[strip, :], ch_ref[:, band], preferred_element_type=f32)
+            )
+            tile = block_ref[strip, band] - product
+            tiles[j, pl.ds(q * spread, spread)] = tile.reshape(spread, groups, 8, TILE)
+
+        if j == 0:
+            pl.semaphore_wait(barrier, cols + rows - 2)
+            for o in range(1, cols):
+                copy = remote(
+                    code_ref, codes.at[o], code_send.at[o], code_recv.at[o], z, lax.rem(d + o, cols)
+                )
+                copy.start()
+                code_copies[o] = copy
+                started.append(copy)
+        for o in range(1, cols):
+            other = lax.rem(d + o, cols)
+            copy = remote(
+                tiles.at[j, other], landed.at[j, o], tile_send.at[j, o], tile_recv.at[j, o], z, other
+            )
+            copy.start()
+            tile_copies[j, o] = copy
+            started.append(copy)
+
+    for o in range(1, cols):
+        code_copies[o].wait_recv()
+    row_copies = []
+    step = min(4, groups)
+    for j in range(rows):
+        p = lax.rem(z + 1 + j, rows)
+        for o in range(1, cols):
+            tile_copies[j, o].wait_recv()
+
+        @pl.loop(0, groups // step)
+        def _(i, j=j, p=p):
+            span = pl.ds(i * step, step)
+            sums = {}
+            for o in range(cols):
+                x = tiles[j, d, span] if o == 0 else landed[j, o, span]
+                code = code_ref if o == 0 else codes.at[o]
+                row_code, col_code = code[p], code[mine]
+                for t in range(slots):
+                    for s in range(slots):
+                        here = (row_code == float(s)) & (col_code == float(t))
+                        term = jnp.where(here[None], x, 0.0)
+                        sums[t, s] = sums[t, s] + term if o else term
+            for t in range(slots):
+                for s in range(slots):
+                    acc[j, t, s, span] = sums[t, s]
+
+        if j < rows - 1:
+            copy = remote(acc.at[j], row_landed.at[j], row_send.at[j], row_recv.at[j], p, d)
+            copy.start()
+            row_copies.append(copy)
+            started.append(copy)
+
+    for copy in row_copies:
+        copy.wait_recv()
+    for t in range(slots):
+        for s in range(slots):
+
+            @pl.loop(0, groups // step)
+            def _(i, t=t, s=s):
+                span = pl.ds(i * step, step)
+                value = acc[rows - 1, t, s, span]
+                for j in range(rows - 1):
+                    value = value + row_landed[j, t, s, span]
+                final[0, t, s, span] = value
+
+    all_copies = []
+    for o in range(1, rows):
+        other = lax.rem(mine + o, rows) * spread + k
+        copy = remote(final.at[0], final.at[o], all_send.at[o], all_recv.at[o], z, other)
+        copy.start()
+        all_copies.append(copy)
+        started.append(copy)
+    for copy in all_copies:
+        copy.wait_recv()
+
+    def column(u, c):
+        place = place_ref[u * cols + c]
+        value = None
+        for o in range(rows):
+            owner = lax.rem(mine - o + rows, rows)
+            for t in range(slots):
+                here = place == (owner + t * rows).astype(jnp.float32)
+                term = jnp.where(here[None, None], final[o, t], 0.0)
+                value = term if value is None else value + term
+        return value
+
+    pair_copies = {}
+    for n in range(1, spread):
+        other = mine * spread + lax.rem(k + n, spread)
+        for u in range(own_cols):
+            stage[n, u] = column(u, other)
+        copy = remote(stage.at[n], pair_landed.at[n], pair_send.at[n], pair_recv.at[n], z, other)
+        copy.start()
+        pair_copies[n] = copy
+        started.append(copy)
+    for u in range(own_cols):
+        out_ref[u, :, k] = column(u, d)
+    for n in range(1, spread):
+        pair_copies[n].wait_recv()
+        source = lax.rem(k - n + spread, spread)
+        for u in range(own_cols):
+            out_ref[u, :, source] = pair_landed[n, u]
+    for copy in started:
+        copy.wait_send()
+
+
+def split(x):
+    high = lax.reduce_precision(x, 8, 7)
+    return high.astype(jnp.bfloat16), (x - high).astype(jnp.bfloat16)
+
+
+def on_device(inverse_interior, coupling, interface_block, iface_ids, row_place, col_place):
+    f32 = jnp.float32
+    rows = lax.axis_size("row")
+    cols = lax.axis_size("col")
+    count = coupling.shape[3] // TILE
+    if rows != count:
+        return general(inverse_interior, coupling, interface_block, iface_ids, row_place, col_place)
+    total_ids = row_place.shape[0]
+    slots = total_ids // rows
+    own_cols = total_ids // cols
+    spread = cols // rows
+    part = TILE // spread
+    groups = part // 8
+    ids = iface_ids[0, 0]
+    matches = ids[:, None] == jnp.arange(total_ids, dtype=jnp.int32)[None, :]
+    pos = jnp.sum(jnp.where(matches, row_place[None, :], 0), axis=1)
+    hit = (pos % rows)[None, :] == jnp.arange(rows, dtype=jnp.int32)[:, None]
+    local = jnp.sum(jnp.where(hit, jnp.arange(count, dtype=jnp.int32)[None, :], 0), axis=1)
+    slot = jnp.sum(jnp.where(hit, pos[None, :] // rows, 0), axis=1)
+    starts = [local[q] * TILE for q in range(rows)]
+
+    def sort(x, axis):
+        return jnp.concatenate([lax.dynamic_slice_in_dim(x, at, TILE, axis) for at in starts], axis)
+
+    c = sort(coupling[0, 0], 1)
+    block = sort(sort(interface_block[0, 0], 0), 1)
+    left = lax.dot_general(
+        c, inverse_interior[0, 0], (((0,), (0,)), ((), ())),
+        precision=lax.Precision.HIGH, preferred_element_type=f32,
+    )
+    th, tl = split(left)
+    ch, cl = split(c)
+    code = jnp.broadcast_to(slot.astype(f32)[:, None, None], (rows, 8, TILE))
+    order = jnp.arange(total_ids, dtype=jnp.int32)
+    place = jnp.sum(jnp.where(order[:, None] == col_place[None, :], row_place[None, :], 0), axis=1)
+    place = jnp.broadcast_to(place.astype(f32)[:, None, None], (total_ids, 8, TILE))
+    vmem = pl.BlockSpec(memory_space=pltpu.VMEM)
+    dma = pltpu.SemaphoreType.DMA
+    out = pl.pallas_call(
+        functools.partial(assemble, rows, cols, slots, own_cols),
+        out_shape=jax.ShapeDtypeStruct((own_cols, slots, spread, groups, 8, TILE), f32),
+        in_specs=[vmem] * 7,
+        out_specs=vmem,
+        scratch_shapes=[
+            pltpu.VMEM((rows, cols, groups, 8, TILE), f32),
+            pltpu.VMEM((rows, cols, groups, 8, TILE), f32),
+            pltpu.VMEM((cols, rows, 8, TILE), f32),
+            pltpu.VMEM((rows, slots, slots, groups, 8, TILE), f32),
+            pltpu.VMEM((rows, slots, slots, groups, 8, TILE), f32),
+            pltpu.VMEM((rows, slots, slots, groups, 8, TILE), f32),
+            pltpu.VMEM((spread, own_cols, slots, groups, 8, TILE), f32),
+            pltpu.VMEM((spread, own_cols, slots, groups, 8, TILE), f32),
+            dma((cols,)), dma((cols,)), dma((rows, cols)), dma((rows, cols)),
+            dma((rows,)), dma((rows,)), dma((rows,)), dma((rows,)), dma((spread,)), dma((spread,)),
+        ],
+        compiler_params=pltpu.CompilerParams(collective_id=0, has_side_effects=True),
+    )(place, code, th, tl, ch, cl, block)
+    return out.reshape(own_cols, slots, TILE, TILE).transpose(1, 2, 0, 3)
+
+
 def solution(mesh):
     return jax.shard_map(
         on_device,

time: 220 us -> 141 us (0.64)
  Pallas kernels: 0 us -> 102 us
  waiting for transfers between devices: 79.3 us -> 0 us
  blocking collectives: 53.3 us -> 0 us
  between operations: 19.4 us -> 2.59 us
  matrix products: 29.7 us -> 17.2 us
  local copies, waits for them, and re-layouts: 19.1 us -> 11.1 us
  starting transfers between devices: 5.27 us -> 0 us
  other arithmetic: 12.6 us -> 8.39 us
    pallas_call x0 -> x1, Pallas kernels: none -> 102 us  [on_device(): pl.pallas_call(functools.partial(assemble, rows, cols, slots, own_cols),...]
    unnamed x1 -> x0, blocking collectives: 53.3 us -> none
    reduce_scatter x1 -> x0, waiting for transfers between devices: 42.5 us -> none  [on_device(): summed = lax.psum_scatter(total, 'row', scatter_dimension=0, tiled=True)[0]]
    all_gather x1 -> x0, waiting for transfers between devices: 36.8 us -> none  [on_device(): gathered = lax.all_gather(summed, 'col')]
    dot_general x2 -> x1, matrix products: 29.7 us -> 17.2 us  [on_device(): lax.dot_general(c, inverse_interior[0, 0], (((0,), (0,)), ((), ())), prec...]
    reduce_sum x4 -> x2, other arithmetic: 6.84 us -> 0.93 us  [the longest x1 0.79 us: on_device(): jnp.sum(jnp.where(order[:, None] == col_place[None, :], row_place[None, :...]
    all_to_all x1 -> x0, starting transfers between devices: 5.22 us -> none  [on_device(): lax.all_to_all(out, 'col', split_axis=0, concat_axis=0, tiled=True)]
    unnamed x17 -> x4, local copies, waits for them, and re-layouts: 6.13 us -> 2.41 us
  transfers between devices with their start and end apart: 3 -> 0, of which waited for: 2 -> 0; matrix products, arithmetic and copies ran while one was open for 1% -> 0% of each run, Pallas kernels for 0% -> 0%
where the time goes in v1:
time: 141 us
  Pallas kernels  102 us (72%)
  matrix products  17.2 us (12%)
  local copies, waits for them, and re-layouts  11.1 us (8%)
  other arithmetic  8.39 us (6%)
  between operations  2.59 us (2%)
    pallas_call x1, Pallas kernels, on_device(): pl.pallas_call(functools.partial(assemble, rows, cols, slots, own_cols),...  102 us
    dot_general x1, matrix products, on_device(): lax.dot_general(c, inverse_interior[0, 0], (((0,), (0,)), ((), ())), prec...  17.2 us
    dynamic_slice x3, local copies, waits for them, and re-layouts, sort(): lax.dynamic_slice_in_dim(x, at, TILE, axis)  4.28 us
    convert_element_type x1, other arithmetic, split(): return (high.astype(jnp.bfloat16), (x - high).astype(jnp.bfloat16))  3.43 us
    concatenate x2, other arithmetic, sort(): jnp.concatenate([lax.dynamic_slice_in_dim(x, at, TILE, axis) for at in st...  3.15 us

profile of v1, /device:TPU:9, one launch (start us, length us, event | category | flops | bytes accessed | tf_op | source)
XLA Modules:
  0.0 141.0 jit_solution(9087465226279107122)
XLA Ops:
  0.0 0.8 select_reduce_fusion
  0.8 0.7 broadcast_in_dim.65.place_ref
  1.5 0.9 select_reduce_fusion.3
  2.4 0.1 select_reduce_fusion.1
  2.5 0.7 broadcast_in_dim.70.code_ref
  3.2 0.7 fusion.5
  6.4 0.0 copy-start.1
  6.4 3.5 %dynamic-slice_bitcast_fusion.3 = (f32[1536,256]{1,0:T(8,128)S(1)}, f32[1536,256]{1,0:T(8,128)S(1)}, f32[1536,256]{1,0:T(8,128)S(1)}, f32[1536,256]{1,0:T(8,128)S(1)}) fusion(f32[1,1,1536,1024]{3,2,1,0:T(8,128)} %param.7, s32[]{:T(128)S(6)} %select_n.62, s32[]{:T(128)S(6)} %select_n.63, s32[]{:T(128)S(6)} %select_n.65, s32[]{:T(128)S(6)} %select_n.64), kind=kLoop, calls=%fused_computation.14 | loop fusion | bytes 12582928 | tf_op jit(solution)/shard_map/dynamic_slice | solution.py:246
  9.9 2.1 %copy-done.1 = f32[1,1,1536,1536]{3,2,1,0:T(8,128)S(1)} copy-done((f32[1,1,1536,1536]{3,2,1,0:T(8,128)S(1)}, f32[1,1,1536,1536]{3,2,1,0:T(8,128)}, u32[]{:S(2)}) %copy-start.1) | copy-done | bytes 9437208
  12.0 17.2 %fusion.2 = (bf16[1024,1536]{1,0:T(8,128)(2,1)}, bf16[1024,1536]{1,0:T(8,128)(2,1)}) fusion(f32[1,1,1536,1536]{3,2,1,0:T(8,128)S(1)} %copy-done.1, f32[1536,256]{1,0:T(8,128)S(1)} %get-tuple-element.13, f32[1536,256]{1,0:T(8,128)S(1)} %get-tuple-element.14, f32[1536,256]{1,0:T(8,128)S(1)} %get-tuple-element.12, f32[1536,256]{1,0:T(8,128)S(1)} %get-tuple-element.11), kind=kOutput, calls=%fused_computation.6 | convolution fusion | flops 14506524672 | bytes 22020096 | tf_op jit(solution)/shard_map/dot_general | solution.py:250
  29.2 0.0 copy-start
  29.2 3.4 %fusion.3 = (bf16[1536,1024]{1,0:T(8,128)(2,1)}, bf16[1536,1024]{1,0:T(8,128)(2,1)}) fusion(f32[1536,256]{1,0:T(8,128)S(1)} %get-tuple-element.13, f32[1536,256]{1,0:T(8,128)S(1)} %get-tuple-element.14, f32[1536,256]{1,0:T(8,128)S(1)} %get-tuple-element.12, f32[1536,256]{1,0:T(8,128)S(1)} %get-tuple-element.11), kind=kLoop, calls=%fused_computation.7 | loop fusion | flops 11010048 | bytes 12582912 | tf_op jit(solution)/shard_map/convert_element_type | solution.py:221
  32.6 0.3 copy-done
  32.9 0.3 dynamic-slice_bitcast_fusion.7
  33.2 0.6 pad_maximum_fusion.1
  33.8 0.5 constant_dynamic-slice_fusion.3
  34.3 2.6 %pad_maximum_fusion.2.block_ref = f32[1024,1024]{1,0:T(8,128)} fusion(f32[1024,256]{1,0:T(8,128)S(1)} %get-tuple-element.16, f32[1024,256]{1,0:T(8,128)S(1)} %get-tuple-element.17, f32[1024,256]{1,0:T(8,128)S(1)} %get-tuple-element.18, f32[1024,256]{1,0:T(8,128)S(1)} %get-tuple-element.15), kind=kLoop, calls=%fused_computation.10 | loop fusion | flops 3145728 | bytes 8388608 | tf_op jit(solution)/shard_map/concatenate | solution.py:246
  36.9 101.7 %shard_map.64 = f32[1,2,2,16,8,256]{5,4,3,2,1,0:T(8,128)} custom-call(f32[8,8,256]{2,1,0:T(8,128)} %broadcast_in_dim.65.place_ref, f32[4,8,256]{2,1,0:T(8,128)} %broadcast_in_dim.70.code_ref, bf16[1024,1536]{1,0:T(8,128)(2,1)} %get-tuple-element.10.th_ref, bf16[1024,1536]{1,0:T(8,128)(2,1)} %get-tuple-element.9.tl_ref, ...), custom_call_target="tpu_custom_call" | custom-call | tf_op jit(solution)/shard_map/pallas_call | solution.py:262
  138.6 2.4 %copy.8 = f32[2,256,1,256]{3,2,1,0:T(1,128)} copy(f32[2,256,1,256]{3,1,0,2:T(8,128)} %bitcast.27) | data formatting | bytes 1048576 | tf_op jit(solution)/shard_map/transpose;reshape | solution.py:281
  (3 shorter events, 0.0 us)
Async XLA Ops:
  6.4 5.6 %copy-start.1 = (f32[1,1,1536,1536]{3,2,1,0:T(8,128)S(1)}, f32[1,1,1536,1536]{3,2,1,0:T(8,128)}, u32[]{:S(2)}) copy-start(f32[1,1,1536,1536]{3,2,1,0:T(8,128)} %param.6) | copy-start | bytes 28311556
  29.2 3.7 %copy-start = (f32[1,1,1024,1024]{3,2,1,0:T(8,128)S(1)}, f32[1,1,1024,1024]{3,2,1,0:T(8,128)}, u32[]{:S(2)}) copy-start(f32[1,1,1024,1024]{3,2,1,0:T(8,128)} %param.8) | copy-start | bytes 12582916
